TPU v7x, 32 devices: a whole 2x2x4 slice. The times are simulated.
32 devices in a mesh: py: 4 (over z), px: 8 (over y, x, core).
Axes of the slice: x: 2, y: 2, z: 4, core: 2. Of those that a mesh axis runs over, the one named last changes fastest.
Arguments:
- residual: bfloat16 [4, 8, 4096, 128], P('py', 'px'), may hold values from -10 to 75
- footprints: bfloat16 [4, 8, 40, 4096], P('py', 'px'), may hold values from 0.049804688 to 1
- traces: bfloat16 [4, 8, 40, 128], P('py', 'px'), may hold values from 0.099609375 to 2
- merge_pairs: int32 [4, 8, 16, 3], P('py', 'px'), may hold values from 0 to 39, as said below
- pair_counts: int32 [4, 8], P('py', 'px'), may hold values from 1 to 16, as said below
- comp_counts: int32 [4, 8], P('py', 'px'), may hold values from 27 to 40, as said below
- row_intersections: int32 [3], replicated, may hold values from 8 to 24
- col_intersections: int32 [7], replicated, may hold values from 8 to 24
Outputs:
- new_footprints: bfloat16 [4, 8, 40, 4096], P('py', 'px')
- new_traces: bfloat16 [4, 8, 40, 128], P('py', 'px')
- correlations: float32 [4, 8, 40, 24], P('py', 'px')
Inputs may be any that keep to these rules, and one draw needn't show every extreme that they name: `merge_pairs`: in slot m < pair_counts[p]: a component id i with 24 <= i < comp_counts[p], a direction d whose neighbour patch exists, and a slot s < 3; ids and (d, s) are distinct within a patch. Later slots are unused. `pair_counts`: at most 3 times the number of neighbours of the patch; some patch has 16. `comp_counts`: at least 24 + pair_counts[p]; components from comp_counts[p] on are unused; some patch has 40.
All inputs are finite; a program needn't handle non-finite values.
Results may differ from a plain program's by a relative error of at most 0.0026.
Values may be sent and summed in bfloat16 or wider, within the bound.
A program may use at most 64 MiB of HBM per device.

v0:
```python
import functools

import jax
import jax.numpy as jnp
from jax import lax
from jax.experimental import pallas as pl
from jax.experimental.pallas import tpu as pltpu
from jax.sharding import PartitionSpec as P

PH = 64
PW = 64
NBR = 3
OV_HI = 24
ITERS = 4
EPS = 1e-05

PAD = 4
STRIP = OV_HI * PW
CHUNK = 512
WIDE = 1024
LANES = 128
STEPS = [(-1, -1), (-1, 0), (-1, 1), (0, -1), (0, 1), (1, -1), (1, 0), (1, 1)]
BF = jnp.bfloat16
F32 = jnp.float32
MESH = pl.DeviceIdType.MESH


def lanes_in(direction, pixels):
    dy = STEPS[direction][0]
    if dy > 0:
        return (0, STRIP)
    if dy < 0:
        return (pixels - STRIP, STRIP)
    return (0, pixels)


def lanes_out(direction, pixels):
    return lanes_in(7 - direction, pixels)


def dot(a, b):
    return jnp.dot(a, b, preferred_element_type=F32)


def dot_t(a, b):
    return lax.dot_general(a, b, (((1,), (1,)), ((), ())), preferred_element_type=F32)


def iota(shape, dim):
    return lax.broadcasted_iota(jnp.int32, shape, dim)


def roll_rows(values, shift):
    rows, count = values.shape
    blocks = count // LANES
    wide = jnp.broadcast_to(shift, (rows, LANES))
    wide = jnp.concatenate([wide] * blocks, axis=0)
    stack = jnp.concatenate([values[:, LANES * b:LANES * (b + 1)] for b in range(blocks)], axis=0)

    def later(x, steps):
        return jnp.concatenate([x[(blocks - steps) * rows:], x[:(blocks - steps) * rows]], axis=0)

    bit = 0
    while (1 << bit) < LANES:
        stack = jnp.where(((wide >> bit) & 1) == 1, pltpu.roll(stack, 1 << bit, 1), stack)
        bit += 1
    stack = jnp.where(iota(stack.shape, 1) < (wide & (LANES - 1)), later(stack, 1), stack)
    while (1 << bit) < count:
        stack = jnp.where(((wide >> bit) & 1) == 1, later(stack, (1 << bit) // LANES), stack)
        bit += 1
    return jnp.concatenate([stack[rows * b:rows * (b + 1)] for b in range(blocks)], axis=1)


def narrow(x):
    return functools.reduce(jnp.add, [x[:, b:b + LANES] for b in range(0, x.shape[1], LANES)])


def shift_of(direction, up, down, left, right):
    flat = direction + (direction >= 4).astype(jnp.int32)
    row = (flat >= 3).astype(jnp.int32) + (flat >= 6).astype(jnp.int32)
    dy = row - 1
    dx = flat - 3 * row - 1
    oy = jnp.where(dy < 0, up - PH, jnp.where(dy > 0, PH - down, 0))
    ox = jnp.where(dx < 0, left - PW, jnp.where(dx > 0, PW - right, 0))
    return oy, ox


def inside_of(oy, ox, first, count):
    pixel = iota((1, count), 1) + first
    y = (pixel >> 6) - oy
    x = (pixel & (PW - 1)) - ox
    return (y >= 0) & (y < PH) & (x >= 0) & (x < PW)


def kernel(
    rows, cols,
    res_hbm, foot_hbm, trace_hbm, pair_hbm, pair_count, comp_count, row_hbm, col_hbm,
    out_foot, out_trace, out_corr,
    res_ref, foot_ref, trace_ref, pair_ref, row_ref, col_ref, sem_in,
    send1, recv1, send2, recv2, send3, recv3,
    border, border_trace, back, back_trace, a_own, a_rem, shape,
    sem_s, sem_r,
):
    pixels = foot_ref.shape[1]
    frames = trace_ref.shape[1]
    comps = foot_ref.shape[0]
    slots = pair_ref.shape[2]
    nb = 8 * NBR
    nbp = 8 * PAD
    my_r = lax.axis_index("py")
    my_c = lax.axis_index("px")

    def target(d):
        return (my_r + STEPS[d][0], my_c + STEPS[d][1])

    def exists(d):
        r, c = target(d)
        return (r >= 0) & (r < rows) & (c >= 0) & (c < cols)

    fetches = [
        (trace_hbm, trace_ref),
        (foot_hbm.at[pl.ds(0, nb)], foot_ref.at[pl.ds(0, nb)]),
        (pair_hbm, pair_ref),
        (row_hbm, row_ref), (col_hbm, col_ref),
        (foot_hbm.at[pl.ds(nb, comps - nb)], foot_ref.at[pl.ds(nb, comps - nb)]),
        (res_hbm, res_ref),
    ]
    fetches = [pltpu.make_async_copy(a, b, sem_in.at[i]) for i, (a, b) in enumerate(fetches)]
    for fetch in fetches:
        fetch.start()
    barrier = pltpu.get_barrier_semaphore()
    for d in range(8):
        @pl.when(exists(d))
        def _():
            pl.semaphore_signal(barrier, 1, device_id=target(d), device_id_type=MESH)

    def copy1(d):
        width = lanes_out(d, pixels)[1] + frames
        return pltpu.make_async_remote_copy(
            send1.at[d, :, pl.ds(0, width)], recv1.at[7 - d, :, pl.ds(0, width)],
            sem_s.at[0, d], sem_r.at[0, 7 - d], device_id=target(d), device_id_type=MESH)

    def copy2(d):
        width = lanes_in(d, pixels)[1]
        return pltpu.make_async_remote_copy(
            send2.at[d, :, pl.ds(0, width)], recv2.at[7 - d, :, pl.ds(0, width)],
            sem_s.at[1, d], sem_r.at[1, 7 - d], device_id=target(d), device_id_type=MESH)

    def copy3(d):
        return pltpu.make_async_remote_copy(
            send3.at[d], recv3.at[7 - d],
            sem_s.at[2, d], sem_r.at[2, 7 - d], device_id=target(d), device_id_type=MESH)

    def arrive(copy, d):
        return copy(7 - d)

    j = iota((nbp, nb), 0)
    pick = (((j & (PAD - 1)) < NBR) & (iota((nbp, nb), 1) == NBR * (j >> 2) + (j & (PAD - 1)))).astype(BF)
    border[...] = jnp.zeros_like(border)
    border_trace[...] = jnp.zeros_like(border_trace)
    back[...] = jnp.zeros_like(back)
    back_trace[...] = jnp.zeros_like(back_trace)
    fetches[0].wait()
    own_traces = trace_ref[...]
    packed_traces = dot(pick, own_traces[0:nb])
    for d in range(8):
        start, width = lanes_out(d, pixels)
        send1[d, :, width:width + frames] = packed_traces[PAD * d:PAD * d + PAD].astype(BF)
    fetches[1].wait()
    for first in range(0, pixels, CHUNK):
        part = dot(pick, foot_ref[0:nb, first:first + CHUNK])
        for d in range(8):
            start, width = lanes_out(d, pixels)
            if start <= first < start + width:
                send1[d, :, first - start:first - start + CHUNK] = part[PAD * d:PAD * d + PAD].astype(BF)

    total = jnp.int32(0)
    for d in range(8):
        total = total + exists(d).astype(jnp.int32)
    pl.semaphore_wait(barrier, total)
    for d in (0, 2, 5, 7, 1, 6, 3, 4):
        @pl.when(exists(d))
        def _():
            copy1(d).start()

    for fetch in fetches[2:]:
        fetch.wait()
    same = iota((slots, slots), 0) == iota((slots, slots), 1)

    def column(values):
        wide = jnp.where(same, values.astype(F32), 0.0)
        return jnp.sum(wide, axis=1, keepdims=True).astype(jnp.int32)

    ids = column(pair_ref[0])
    direction = column(pair_ref[1])
    place = column(pair_ref[2])
    live = iota((slots, 1), 0) < pair_count[0, 0]
    own_hot = ((iota((slots, comps), 1) == ids) & live).astype(BF)
    border_slot = PAD * direction + place
    border_hot = ((iota((slots, nbp), 1) == border_slot) & live).astype(BF)
    up = row_ref[jnp.clip(my_r - 1, 0, rows - 2)]
    down = row_ref[jnp.clip(my_r, 0, rows - 2)]
    left = col_ref[jnp.clip(my_c - 1, 0, cols - 2)]
    right = col_ref[jnp.clip(my_c, 0, cols - 2)]
    oy, ox = shift_of(direction, up, down, left, right)
    go = (oy * PW + ox) & (pixels - 1)
    come = (-(oy * PW + ox)) & (pixels - 1)

    c_own = dot(own_hot, own_traces)
    c_own_bf = c_own.astype(BF)
    energy = jnp.sum(c_own * c_own, axis=1, keepdims=True)
    for first in range(0, pixels, CHUNK):
        span = slice(first, first + CHUNK)
        mine = dot(own_hot, foot_ref[:, span])
        a_own[:, span] = mine
        shape[:, span] = dot_t(c_own_bf, res_ref[span, :]) + mine * energy

    for d in range(8):
        start, width = lanes_in(d, pixels)

        @pl.when(exists(d))
        def _():
            arrive(copy1, d).wait_recv()
            border[PAD * d:PAD * d + PAD, start:start + width] = recv1[d, :, 0:width]
            border_trace[PAD * d:PAD * d + PAD, :] = recv1[d, :, width:width + frames]

    c_rem = dot(border_hot, border_trace[...])
    for first in range(0, pixels, CHUNK):
        span = slice(first, first + CHUNK)
        a_rem[:, span] = dot(border_hot, border[:, span])
    for low in range(0, slots, 8):
        part = slice(low, low + 8)
        moved = roll_rows(a_rem[part, :], go[part])
        a_rem[part, :] = jnp.where(inside_of(oy[part], ox[part], 0, pixels), moved, 0.0)

    trace = c_own
    for t in range(ITERS):
        with_own = jnp.sum(c_own * trace, axis=1, keepdims=True)
        with_rem = jnp.sum(c_rem * trace, axis=1, keepdims=True)
        norm = 1.0 / (jnp.sum(trace * trace, axis=1, keepdims=True) + EPS * frames)
        trace_bf = trace.astype(BF)
        down_sum = jnp.zeros((slots, frames), F32)
        sum_own = jnp.zeros((slots, LANES), F32)
        sum_rem = jnp.zeros((slots, LANES), F32)
        sum_sq = jnp.zeros((slots, LANES), F32)
        for first in range(0, pixels, WIDE):
            span = slice(first, first + WIDE)
            mine = a_own[:, span]
            theirs = a_rem[:, span]
            if t == 0:
                across = shape[:, span]
            else:
                across = dot_t(trace_bf, res_ref[span, :]) + mine * with_own
            foot = jnp.maximum(across + theirs * with_rem, 0.0) * norm
            shape[:, span] = foot
            sum_own = sum_own + narrow(mine * foot)
            sum_rem = sum_rem + narrow(theirs * foot)
            sum_sq = sum_sq + narrow(foot * foot)
            if t < ITERS - 1:
                down_sum = down_sum + dot(foot.astype(BF), res_ref[span, :])
        if t == ITERS - 1:
            row = iota((nbp, 1), 0)
            home_y, home_x = shift_of(row >> 2, up, down, left, right)
            home_hot_t = border_hot
            hit = lax.dot_general(home_hot_t, jnp.ones((slots, 128), BF), (((0,), (0,)), ((), ())),
                                  preferred_element_type=F32)[:, 0:1] > 0.5
            for low in range(0, slots, 8):
                part = slice(low, low + 8)
                back[part, :] = roll_rows(shape[part, :], come[part]).astype(BF)
            for d in range(8):
                start, width = lanes_in(d, pixels)
                base = 2 * PAD * (d // 2)
                low = PAD * (d % 2)
                sent = lax.dot_general(
                    home_hot_t[:, base:base + 2 * PAD], back[0:slots, start:start + width],
                    (((0,), (0,)), ((), ())), preferred_element_type=F32)
                part = slice(base, base + 2 * PAD)
                ok = inside_of(-home_y[part], -home_x[part], start, width) & hit[part]
                kept = border[2 * PAD * (d // 2):2 * PAD * (d // 2) + 2 * PAD, start:start + width].astype(F32)
                sent = jnp.where(ok, sent, kept)
                send2[d, :, 0:width] = sent[low:low + PAD].astype(BF)
            for d in (0, 2, 5, 7, 1, 6, 3, 4):
                @pl.when(exists(d))
                def _():
                    copy2(d).start()
            back[...] = jnp.zeros_like(back)
            for first in range(0, pixels, WIDE):
                span = slice(first, first + WIDE)
                down_sum = down_sum + dot(shape[:, span].astype(BF), res_ref[span, :])
        dot_own = jnp.sum(sum_own, axis=1, keepdims=True)
        dot_rem = jnp.sum(sum_rem, axis=1, keepdims=True)
        scale = 1.0 / (jnp.sum(sum_sq, axis=1, keepdims=True) + EPS * pixels)
        trace = jnp.maximum(down_sum + c_own * dot_own + c_rem * dot_rem, 0.0) * scale

    trace_bf = trace.astype(BF)
    sent = lax.dot_general(border_hot, trace_bf, (((0,), (0,)), ((), ())), preferred_element_type=F32)
    sent = jnp.where(hit, sent, border_trace[...].astype(F32))
    for d in range(8):
        send3[d] = sent[PAD * d:PAD * d + PAD].astype(BF)
    for d in (0, 2, 5, 7, 1, 6, 3, 4):
        @pl.when(exists(d))
        def _():
            copy3(d).start()

    alive = iota((comps, 1), 0) < comp_count[0, 0]
    upper = slice(nb, comps)
    hot_up = own_hot[:, upper]
    ones = jnp.ones((slots, 128), BF)
    hit_up = lax.dot_general(hot_up, ones, (((0,), (0,)), ((), ())), preferred_element_type=F32)[:, 0:1] > 0.5
    alive_up = alive[upper]
    for first in range(0, pixels, CHUNK):
        span = slice(first, first + CHUNK)
        new = lax.dot_general(hot_up, shape[:, span].astype(BF), (((0,), (0,)), ((), ())),
                              preferred_element_type=F32)
        new = jnp.where(hit_up, new, foot_ref[upper, span].astype(F32))
        out_foot[upper, span] = jnp.where(alive_up, new, 0.0).astype(BF)
    new = lax.dot_general(hot_up, trace_bf, (((0,), (0,)), ((), ())), preferred_element_type=F32)
    new = jnp.where(hit_up, new, own_traces[upper].astype(F32))
    out_trace[upper, :] = jnp.where(alive_up, new, 0.0).astype(BF)

    k = iota((nb, nbp), 0)
    k_dir = iota((nb, 1), 0)
    dir_of = jnp.zeros((nb, 1), jnp.int32)
    dir_wide = jnp.zeros((nb, nbp), jnp.int32)
    for d in range(1, 8):
        dir_of = dir_of + (k_dir >= NBR * d).astype(jnp.int32)
        dir_wide = dir_wide + (k >= NBR * d).astype(jnp.int32)
    squeeze = (iota((nb, nbp), 1) == PAD * dir_wide + k - NBR * dir_wide).astype(BF)
    local = own_traces.astype(F32)
    local = local - jnp.mean(local, axis=1, keepdims=True)
    remote = dot(squeeze, border_trace[...])
    remote = remote - jnp.mean(remote, axis=1, keepdims=True)
    spread_remote = jnp.mean(remote * remote, axis=1, keepdims=True)
    full = functools.partial(lax.dot_general, dimension_numbers=(((1,), (1,)), ((), ())),
                             precision=lax.Precision.HIGHEST, preferred_element_type=F32)
    cov = full(remote, local) / frames
    spread_local = full(jnp.ones((8, frames), F32), local * local)[0:1] / frames
    corr = cov / jnp.sqrt((spread_local + EPS) * (spread_remote + EPS))
    out_corr[...] = jnp.where(iota((1, comps), 1) < comp_count[0, 0], corr, 0.0)

    for d in range(8):
        start, width = lanes_out(d, pixels)

        @pl.when(exists(d))
        def _():
            arrive(copy2, d).wait_recv()
            back[PAD * d:PAD * d + PAD, start:start + width] = recv2[d, :, 0:width]
    for d in range(8):
        @pl.when(exists(d))
        def _():
            arrive(copy3, d).wait_recv()
            back_trace[PAD * d:PAD * d + PAD, :] = recv3[d]

    flat = dir_of + (dir_of >= 4).astype(jnp.int32)
    row = (flat >= 3).astype(jnp.int32) + (flat >= 6).astype(jnp.int32)
    dy = row - 1
    dx = flat - 3 * row - 1
    there = (my_r + dy >= 0) & (my_r + dy < rows) & (my_c + dx >= 0) & (my_c + dx < cols)
    alive_low = alive[0:nb]
    for first in range(0, pixels, CHUNK):
        span = slice(first, first + CHUNK)
        new = dot(squeeze, back[:, span])
        use = there
        if first < pixels - STRIP:
            use = use & (dy <= 0)
        if first + CHUNK > STRIP:
            use = use & (dy >= 0)
        new = jnp.where(use, new, foot_ref[0:nb, span].astype(F32))
        out_foot[0:nb, span] = jnp.where(alive_low, new, 0.0).astype(BF)
    new = dot(squeeze, back_trace[...])
    new = jnp.where(there, new, own_traces[0:nb].astype(F32))
    out_trace[0:nb, :] = jnp.where(alive_low, new, 0.0).astype(BF)

    for d in range(8):
        @pl.when(exists(d))
        def _():
            copy1(d).wait_send()
            copy2(d).wait_send()
            copy3(d).wait_send()


def store(foot, trace, corr, out_foot, out_trace, out_corr, sem):
    pairs = ((foot, out_foot), (trace, out_trace), (corr, out_corr))
    copies = [pltpu.make_async_copy(a, b, sem.at[i]) for i, (a, b) in enumerate(pairs)]
    for copy in copies:
        copy.start()
    for copy in copies:
        copy.wait()


def shards(rows, cols, residual, footprints, traces, merge_pairs, pair_counts, comp_counts, row_int, col_int):
    pixels, frames = residual.shape[2:]
    comps = footprints.shape[2]
    slots = merge_pairs.shape[2]
    nb, nbp = 8 * NBR, 8 * PAD
    vmem = pl.BlockSpec(memory_space=pltpu.VMEM)
    smem = pl.BlockSpec(memory_space=pltpu.SMEM)
    hbm = pl.BlockSpec(memory_space=pltpu.HBM)
    i32 = jnp.int32
    block = pltpu.VMEM((8, PAD, pixels), BF)
    block_t = pltpu.VMEM((8, PAD, frames), BF)
    both = pltpu.VMEM((8, PAD, pixels + frames), BF)
    pairs = jnp.transpose(merge_pairs, (0, 3, 1, 2))[0]
    out_shape = (
        jax.ShapeDtypeStruct((comps, pixels), BF),
        jax.ShapeDtypeStruct((comps, frames), BF),
        jax.ShapeDtypeStruct((nb, comps), F32),
    )
    results = pl.pallas_call(
        functools.partial(kernel, rows, cols),
        out_shape=out_shape,
        in_specs=[hbm] * 4 + [smem] * 2 + [hbm] * 2,
        out_specs=(vmem,) * 3,
        scratch_shapes=[
            pltpu.VMEM((pixels, frames), BF), pltpu.VMEM((comps, pixels), BF), pltpu.VMEM((comps, frames), BF),
            pltpu.VMEM((3, 1, slots), i32),
            pltpu.SMEM(row_int.shape, i32), pltpu.SMEM(col_int.shape, i32), pltpu.SemaphoreType.DMA((9,)),
            both, both, block, block, block_t, block_t,
            pltpu.VMEM((nbp, pixels), BF), pltpu.VMEM((nbp, frames), BF),
            pltpu.VMEM((nbp, pixels), BF), pltpu.VMEM((nbp, frames), BF),
            pltpu.VMEM((slots, pixels), F32), pltpu.VMEM((slots, pixels), F32),
            pltpu.VMEM((slots, pixels), F32),
            pltpu.SemaphoreType.DMA((3, 8)), pltpu.SemaphoreType.DMA((3, 8)),
        ],
        compiler_params=pltpu.CompilerParams(
            collective_id=0, has_side_effects=True, vmem_limit_bytes=32 * 1024 * 1024),
    )(*[pltpu.with_memory_space_constraint(x, pltpu.HBM) for x in (
        residual[0, 0], footprints[0, 0], traces[0, 0], pairs)], pair_counts, comp_counts,
      *[pltpu.with_memory_space_constraint(x, pltpu.HBM) for x in (row_int, col_int)])
    foot, trace, corr = pl.pallas_call(
        store,
        out_shape=out_shape,
        in_specs=[vmem] * 3,
        out_specs=(hbm,) * 3,
        scratch_shapes=[pltpu.SemaphoreType.DMA((3,))],
        compiler_params=pltpu.CompilerParams(vmem_limit_bytes=4 * 1024 * 1024),
    )(*results)
    return foot[None, None], trace[None, None], jnp.transpose(corr)[None, None]


def solution(mesh):
    rows, cols = mesh.shape["py"], mesh.shape["px"]
    spec = P("py", "px", None, None)
    return jax.shard_map(
        functools.partial(shards, rows, cols), mesh=mesh,
        in_specs=(spec, spec, spec, spec, P("py", "px"), P("py", "px"), P(), P()),
        out_specs=(spec, spec, spec), check_vma=False)
```

profile of v0, /device:TPU:1, one launch (start us, length us, event | category | flops | bytes accessed | tf_op | source)
XLA Modules:
  0.0 18.4 jit_solution(14471597086343349563)
XLA Ops:
  1.9 15.7 %shard_map.103 = (bf16[40,4096]{1,0:T(8,128)(2,1)S(1)}, bf16[40,128]{1,0:T(8,128)(2,1)S(1)}, f32[24,40]{1,0:T(8,128)S(1)}) custom-call(bf16[4096,128]{1,0:T(8,128)(2,1)} %bitcast.11, bf16[40,4096]{1,0:T(8,128)(2,1)} %bitcast.12, bf16[40,128]{1,0:T(8,128)(2,1)} %bitcast.13, s32[3,1,16]{2,1,0:T(1,128)} %bitcast.14, s32[1,1]{1,0:T(1,128)S(6)} %copy.11.pair_count, ...), custom_call_target="tpu_custom_call" | custom-call | tf_op jit(solution)/shard_map/pallas_call | solution.py:409
  17.6 0.8 %shard_map.104 = (bf16[40,4096]{1,0:T(8,128)(2,1)}, bf16[40,128]{1,0:T(8,128)(2,1)}, f32[24,40]{1,0:T(8,128)}) custom-call(bf16[40,4096]{1,0:T(8,128)(2,1)S(1)} %get-tuple-element.9.foot, bf16[40,128]{1,0:T(8,128)(2,1)S(1)} %get-tuple-element.10.trace, f32[24,40]{1,0:T(8,128)S(1)} %get-tuple-element.11.corr), custom_call_target="tpu_custom_call" | custom-call | tf_op jit(solution)/shard_map/pallas_call | solution.py:430
where the time goes:
time: 18.7 us; the launch traced here: 18.4 us
  Pallas kernels  16.5 us (88%)
  between operations  1.93 us (10%)
    pallas_call x1, Pallas kernels, shards(): pl.pallas_call(functools.partial(kernel, rows, cols), out_shape=out_shape...  15.7 us
    pallas_call x1, Pallas kernels, shards(): pl.pallas_call(store, out_shape=out_shape, in_specs=[vmem] * 3, out_specs...  0.76 us

commit v1 on v0

v1 whole, which is shorter than its diff:
```python
import functools

import jax
import jax.numpy as jnp
from jax import lax
from jax.experimental import pallas as pl
from jax.experimental.pallas import tpu as pltpu
from jax.sharding import PartitionSpec as P

PH = 64
PW = 64
NBR = 3
OV_HI = 24
ITERS = 4
EPS = 1e-05

PAD = 4
STRIP = OV_HI * PW
CHUNK = 512
WIDE = 1024
LANES = 128
LOW = (PH - OV_HI) // 2
ORDER = (0, 2, 5, 7, 1, 6, 3, 4)
RECEIVE = (3, 4, 1, 6, 0, 2, 5, 7)
STEPS = [(-1, -1), (-1, 0), (-1, 1), (0, -1), (0, 1), (1, -1), (1, 0), (1, 1)]
BF = jnp.bfloat16
F32 = jnp.float32
MESH = pl.DeviceIdType.MESH


def lanes_in(direction, pixels):
    dy = STEPS[direction][0]
    if dy > 0:
        return (0, STRIP)
    if dy < 0:
        return (pixels - STRIP, STRIP)
    return (0, pixels)


def lanes_out(direction, pixels):
    return lanes_in(7 - direction, pixels)


def dot(a, b):
    return jnp.dot(a, b, preferred_element_type=F32)


def dot_t(a, b):
    return lax.dot_general(a, b, (((1,), (1,)), ((), ())), preferred_element_type=F32)


def iota(shape, dim):
    return lax.broadcasted_iota(jnp.int32, shape, dim)


def narrow(x):
    return functools.reduce(jnp.add, [x[:, b:b + LANES] for b in range(0, x.shape[1], LANES)])


def shift_of(direction, up, down, left, right):
    flat = direction + (direction >= 4).astype(jnp.int32)
    row = (flat >= 3).astype(jnp.int32) + (flat >= 6).astype(jnp.int32)
    dy = row - 1
    dx = flat - 3 * row - 1
    oy = jnp.where(dy < 0, up - PH, jnp.where(dy > 0, PH - down, 0))
    ox = jnp.where(dx < 0, left - PW, jnp.where(dx > 0, PW - right, 0))
    return oy, ox


def inside_of(oy, ox, first, count):
    pixel = iota((1, count), 1) + first
    y = (pixel >> 6) - oy
    x = (pixel & (PW - 1)) - ox
    return (y >= 0) & (y < PH) & (x >= 0) & (x < PW)


def kernel(
    rows, cols,
    res_hbm, foot_hbm, trace_hbm, pair_hbm, pair_count, comp_count, row_hbm, col_hbm,
    out_foot, out_trace, out_corr,
    res_ref, foot_ref, trace_ref, pair_ref, row_ref, col_ref, sem_in,
    send, recv1, recv2, wide, res_t,
    border, border_trace, back, back_trace, a_own, a_rem, shape, take, keep,
    sem_s, sem_r,
):
    pixels = foot_ref.shape[1]
    frames = trace_ref.shape[1]
    comps = foot_ref.shape[0]
    slots = pair_ref.shape[2]
    nb = 8 * NBR
    nbp = 8 * PAD
    my_r = lax.axis_index("py")
    my_c = lax.axis_index("px")

    def target(d):
        return (my_r + STEPS[d][0], my_c + STEPS[d][1])

    def exists(d):
        r, c = target(d)
        return (r >= 0) & (r < rows) & (c >= 0) & (c < cols)

    barrier = pltpu.get_barrier_semaphore()
    for d in range(8):
        @pl.when(exists(d))
        def _():
            pl.semaphore_signal(barrier, 1, device_id=target(d), device_id_type=MESH)
    fetches = [
        (trace_hbm, trace_ref),
        (row_hbm, row_ref), (col_hbm, col_ref),
        (foot_hbm.at[pl.ds(0, nb)], foot_ref.at[pl.ds(0, nb)]),
        (pair_hbm, pair_ref),
        (foot_hbm.at[pl.ds(nb, comps - nb)], foot_ref.at[pl.ds(nb, comps - nb)]),
        (res_hbm, res_ref),
    ]
    fetches = [pltpu.make_async_copy(a, b, sem_in.at[i]) for i, (a, b) in enumerate(fetches)]
    for fetch in fetches:
        fetch.start()

    def span1(d):
        return lanes_in(d, pixels)[1] + frames

    def remote(src, dst, d, phase):
        return pltpu.make_async_remote_copy(
            src, dst, sem_s.at[d], sem_r.at[phase, 7 - d],
            device_id=target(d), device_id_type=MESH)

    def copy1(d):
        part = pl.ds(0, span1(d))
        return remote(send.at[d, :, part], recv1.at[7 - d, :, part], d, 0)

    def copy2(d):
        width = lanes_in(d, pixels)[1]
        return remote(send.at[d, :, pl.ds(span1(d), width)], recv2.at[7 - d, :, pl.ds(0, width)], d, 1)

    def copy3(d):
        width = lanes_in(d, pixels)[1]
        return remote(send.at[d, :, pl.ds(span1(d) + width, frames)],
                      recv2.at[7 - d, :, pl.ds(width, frames)], d, 1)

    def both(d):
        part = pl.ds(0, span1(d))
        return remote(send.at[d, :, part], recv2.at[7 - d, :, part], d, 1)

    def all_sent(d):
        part = send.at[d, :, pl.ds(0, 2 * span1(d))]
        return remote(part, part, d, 1)

    j = iota((nbp, nb), 0)
    pick = (((j & (PAD - 1)) < NBR) & (iota((nbp, nb), 1) == NBR * (j >> 2) + (j & (PAD - 1)))).astype(BF)
    border[...] = jnp.zeros_like(border)
    border_trace[...] = jnp.zeros_like(border_trace)
    back[...] = jnp.zeros_like(back)
    back_trace[...] = jnp.zeros_like(back_trace)
    fetches[0].wait()
    own_traces = trace_ref[...]
    packed_traces = dot(pick, own_traces[0:nb])
    for d in range(8):
        width = lanes_in(d, pixels)[1]
        send[d, :, width:width + frames] = packed_traces[PAD * d:PAD * d + PAD].astype(BF)
    fetches[1].wait()
    fetches[2].wait()
    up = row_ref[jnp.clip(my_r - 1, 0, rows - 2)]
    down = row_ref[jnp.clip(my_r, 0, rows - 2)]
    left = col_ref[jnp.clip(my_c - 1, 0, cols - 2)]
    right = col_ref[jnp.clip(my_c, 0, cols - 2)]

    def offsets(d):
        dy, dx = STEPS[d]
        oy = up - PH if dy < 0 else PH - down if dy > 0 else 0
        ox = left - PW if dx < 0 else PW - right if dx > 0 else 0
        return oy, ox

    def slide(part, dy):
        count = STRIP // LANES
        base = (pixels - STRIP) if dy > 0 else 0
        oy = offsets(6 if dy > 0 else 1)[0]
        steps = (oy >> 1) - LOW if dy > 0 else 0 - LOW - (oy >> 1)
        stack = jnp.concatenate([wide[part, base + LANES * b:base + LANES * (b + 1)] for b in range(count)], axis=0)
        stack = jnp.concatenate([stack, stack[8 * (count - 1):]], axis=0)
        for bit in (3, 2, 1, 0):
            jump = 8 << bit
            chosen = jnp.broadcast_to(((steps >> bit) & 1) == 1, (8 * count + 8 - jump, LANES))
            if dy > 0:
                moved = jnp.where(chosen, stack[jump:], stack[:-jump])
                stack = jnp.concatenate([moved, stack[-jump:]], axis=0)
            else:
                moved = jnp.where(chosen, stack[:-jump], stack[jump:])
                stack = jnp.concatenate([stack[:jump], moved], axis=0)
        return stack

    def emit(d, first, masked, slid):
        oy, ox = offsets(d)
        dy, dx = STEPS[d]
        start, width = lanes_in(d, pixels)
        blocks = width // LANES
        part = slice(8 * (d // 2), 8 * (d // 2) + 8)
        low = PAD * (d % 2)
        if dy == 0:
            stack = jnp.concatenate([wide[part, LANES * b:LANES * (b + 1)] for b in range(blocks)], axis=0)
            stack = pltpu.roll(stack, (0 - ox) & (LANES - 1), 1)
        else:
            if (d // 2, dy) not in slid:
                slid[d // 2, dy] = slide(part, dy)
            odd = oy & 1
            stack = pltpu.roll(slid[d // 2, dy], (0 - ox - PW * odd) & (LANES - 1), 1)
            later = (iota((8 * blocks, LANES), 1) >= PW * (2 - odd))
            stack = jnp.where(later, stack[8:], stack[:-8])
        if masked:
            lane = iota((8 * blocks, LANES), 1)
            y = (start >> 6) + 2 * (iota((8 * blocks, LANES), 0) >> 3) + (lane >> 6) + oy
            x = (lane & (PW - 1)) + ox
            stack = jnp.where((y >= 0) & (y < PH) & (x >= 0) & (x < PW), stack, 0.0)
        for b in range(blocks):
            send[d, :, first + LANES * b:first + LANES * (b + 1)] = stack[8 * b + low:8 * b + low + PAD].astype(BF)

    fetches[3].wait()
    for first in range(0, pixels, CHUNK):
        wide[:, first:first + CHUNK] = dot(pick, foot_ref[0:nb, first:first + CHUNK])
    slid = {}
    for d in ORDER:
        emit(d, 0, True, slid)

    total = jnp.int32(0)
    for d in range(8):
        total = total + exists(d).astype(jnp.int32)
    pl.semaphore_wait(barrier, total)
    for d in ORDER:
        @pl.when(exists(d))
        def _():
            copy1(d).start()

    for fetch in fetches[4:]:
        fetch.wait()
    same = iota((slots, slots), 0) == iota((slots, slots), 1)

    def column(values):
        grid = jnp.where(same, values.astype(F32), 0.0)
        return jnp.sum(grid, axis=1, keepdims=True).astype(jnp.int32)

    ids = column(pair_ref[0])
    direction = column(pair_ref[1])
    place = column(pair_ref[2])
    live = iota((slots, 1), 0) < pair_count[0, 0]
    own_hot = ((iota((slots, comps), 1) == ids) & live).astype(BF)
    border_slot = PAD * direction + place
    border_hot = ((iota((slots, nbp), 1) == border_slot) & live).astype(BF)
    hit = lax.dot_general(border_hot, jnp.ones((slots, LANES), BF), (((0,), (0,)), ((), ())),
                          preferred_element_type=F32) > 0.5

    c_own = dot(own_hot, own_traces)
    c_own_bf = c_own.astype(BF)
    energy = jnp.sum(c_own * c_own, axis=1, keepdims=True)
    for first in range(0, pixels, CHUNK):
        span = slice(first, first + CHUNK)
        mine = dot(own_hot, foot_ref[:, span])
        a_own[:, span] = mine
        turned = jnp.transpose(res_ref[span, :])
        res_t[:, span] = turned
        shape[:, span] = dot(c_own_bf, turned) + mine * energy

    k = iota((nb, nbp), 0)
    k_dir = iota((nb, 1), 0)
    dir_of = jnp.zeros((nb, 1), jnp.int32)
    dir_wide = jnp.zeros((nb, nbp), jnp.int32)
    for d in range(1, 8):
        dir_of = dir_of + (k_dir >= NBR * d).astype(jnp.int32)
        dir_wide = dir_wide + (k >= NBR * d).astype(jnp.int32)
    squeeze = (iota((nb, nbp), 1) == PAD * dir_wide + k - NBR * dir_wide).astype(BF)
    alive = iota((comps, 1), 0) < comp_count[0, 0]
    alive_low = alive[0:nb]

    for d in RECEIVE:
        start, width = lanes_out(d, pixels)

        @pl.when(exists(d))
        def _():
            copy1(7 - d).wait_recv()
            border[PAD * d:PAD * d + PAD, start:start + width] = recv1[d, :, 0:width]
            border_trace[PAD * d:PAD * d + PAD, :] = recv1[d, :, width:width + frames]

    c_rem = dot(border_hot, border_trace[...])
    for first in range(0, pixels, CHUNK):
        span = slice(first, first + CHUNK)
        a_rem[:, span] = dot(border_hot, border[:, span])

    trace = c_own
    for t in range(ITERS):
        with_own = jnp.sum(c_own * trace, axis=1, keepdims=True)
        with_rem = jnp.sum(c_rem * trace, axis=1, keepdims=True)
        norm = 1.0 / (jnp.sum(trace * trace, axis=1, keepdims=True) + EPS * frames)
        trace_bf = trace.astype(BF)
        down_sum = jnp.zeros((slots, frames), F32)
        sum_own = jnp.zeros((slots, LANES), F32)
        sum_rem = jnp.zeros((slots, LANES), F32)
        sum_sq = jnp.zeros((slots, LANES), F32)
        for first in range(0, pixels, WIDE):
            span = slice(first, first + WIDE)
            mine = a_own[:, span]
            theirs = a_rem[:, span]
            if t == 0:
                across = shape[:, span]
            else:
                across = dot(trace_bf, res_t[:, span]) + mine * with_own
            foot = jnp.maximum(across + theirs * with_rem, 0.0) * norm
            sum_own = sum_own + narrow(mine * foot)
            sum_rem = sum_rem + narrow(theirs * foot)
            sum_sq = sum_sq + narrow(foot * foot)
            foot = foot.astype(BF)
            down_sum = down_sum + dot(foot, res_ref[span, :])
            if t == ITERS - 1:
                shape[:, span] = foot.astype(F32)
                wide[:, first:first + WIDE] = lax.dot_general(
                    border_hot, foot, (((0,), (0,)), ((), ())), preferred_element_type=F32)
        if t == ITERS - 1:
            slid = {}
            for d in ORDER:
                emit(d, span1(d), False, slid)
            for d in ORDER:
                @pl.when(exists(d))
                def _():
                    copy2(d).start()
        dot_own = jnp.sum(sum_own, axis=1, keepdims=True)
        dot_rem = jnp.sum(sum_rem, axis=1, keepdims=True)
        scale = 1.0 / (jnp.sum(sum_sq, axis=1, keepdims=True) + EPS * pixels)
        trace = jnp.maximum(down_sum + c_own * dot_own + c_rem * dot_rem, 0.0) * scale

    trace_bf = trace.astype(BF)
    sent = lax.dot_general(border_hot, trace_bf, (((0,), (0,)), ((), ())), preferred_element_type=F32)
    sent = jnp.where(hit, sent, -1.0)
    for d in range(8):
        first = span1(d) + lanes_in(d, pixels)[1]
        send[d, :, first:first + frames] = sent[PAD * d:PAD * d + PAD].astype(BF)
    for d in ORDER:
        @pl.when(exists(d))
        def _():
            copy3(d).start()

    upper = slice(nb, comps)
    hot_up = own_hot[:, upper]
    ones = jnp.ones((slots, 128), BF)
    hit_up = lax.dot_general(hot_up, ones, (((0,), (0,)), ((), ())), preferred_element_type=F32)[:, 0:1] > 0.5
    alive_up = alive[upper]
    for first in range(0, pixels, CHUNK):
        span = slice(first, first + CHUNK)
        new = lax.dot_general(hot_up, shape[:, span].astype(BF), (((0,), (0,)), ((), ())),
                              preferred_element_type=F32)
        new = jnp.where(hit_up, new, foot_ref[upper, span].astype(F32))
        out_foot[upper, span] = jnp.where(alive_up, new, 0.0).astype(BF)
    new = lax.dot_general(hot_up, trace_bf, (((0,), (0,)), ((), ())), preferred_element_type=F32)
    new = jnp.where(hit_up, new, own_traces[upper].astype(F32))
    out_trace[upper, :] = jnp.where(alive_up, new, 0.0).astype(BF)

    local = own_traces.astype(F32)
    local = local - jnp.mean(local, axis=1, keepdims=True)
    remote_traces = dot(squeeze, border_trace[...])
    remote_traces = remote_traces - jnp.mean(remote_traces, axis=1, keepdims=True)
    spread_remote = jnp.mean(remote_traces * remote_traces, axis=1, keepdims=True)
    full = functools.partial(lax.dot_general, dimension_numbers=(((1,), (1,)), ((), ())),
                             precision=lax.Precision.HIGHEST, preferred_element_type=F32)
    cov = full(remote_traces, local) / frames
    spread_local = full(jnp.ones((8, frames), F32), local * local)[0:1] / frames
    corr = cov / jnp.sqrt((spread_local + EPS) * (spread_remote + EPS))
    out_corr[...] = jnp.where(iota((1, comps), 1) < comp_count[0, 0], corr, 0.0)

    oy, ox = shift_of(dir_of, up, down, left, right)
    flat = dir_of + (dir_of >= 4).astype(jnp.int32)
    row = (flat >= 3).astype(jnp.int32) + (flat >= 6).astype(jnp.int32)
    dy = row - 1
    dx = flat - 3 * row - 1
    there = (my_r + dy >= 0) & (my_r + dy < rows) & (my_c + dx >= 0) & (my_c + dx < cols) & alive_low
    for first in range(0, pixels, CHUNK):
        span = slice(first, first + CHUNK)
        take[:, span] = jnp.where(inside_of(oy, ox, first, CHUNK) & there, 1.0, 0.0)
        keep[:, span] = jnp.where(alive_low, foot_ref[0:nb, span].astype(F32), 0.0)

    for d in RECEIVE:
        start, width = lanes_out(d, pixels)

        @pl.when(exists(d))
        def _():
            both(7 - d).wait_recv()
            back[PAD * d:PAD * d + PAD, start:start + width] = recv2[d, :, 0:width]
            back_trace[PAD * d:PAD * d + PAD, :] = recv2[d, :, width:width + frames]

    new = dot(squeeze, back_trace[...])
    came = new >= 0.0
    new = jnp.where(there & came, new, jnp.where(alive_low, own_traces[0:nb].astype(F32), 0.0))
    out_trace[0:nb, :] = new.astype(BF)
    came = jnp.where(came, 1.0, 0.0)
    came = jnp.concatenate([came] * (CHUNK // LANES), axis=1)
    for first in range(0, pixels, CHUNK):
        span = slice(first, first + CHUNK)
        new = dot(squeeze, back[:, span])
        out_foot[0:nb, span] = jnp.where(take[:, span] * came > 0.5, new, keep[:, span]).astype(BF)

    for d in range(8):
        @pl.when(exists(d))
        def _():
            all_sent(d).wait_send()


def store(foot, trace, corr, out_foot, out_trace, out_corr, sem):
    pairs = ((foot, out_foot), (trace, out_trace), (corr, out_corr))
    copies = [pltpu.make_async_copy(a, b, sem.at[i]) for i, (a, b) in enumerate(pairs)]
    for copy in copies:
        copy.start()
    for copy in copies:
        copy.wait()


def shards(rows, cols, residual, footprints, traces, merge_pairs, pair_counts, comp_counts, row_int, col_int):
    pixels, frames = residual.shape[2:]
    comps = footprints.shape[2]
    slots = merge_pairs.shape[2]
    nb, nbp = 8 * NBR, 8 * PAD
    vmem = pl.BlockSpec(memory_space=pltpu.VMEM)
    smem = pl.BlockSpec(memory_space=pltpu.SMEM)
    hbm = pl.BlockSpec(memory_space=pltpu.HBM)
    i32 = jnp.int32
    both = pltpu.VMEM((8, PAD, pixels + frames), BF)
    pairs = jnp.transpose(merge_pairs, (0, 3, 1, 2))[0]
    out_shape = (
        jax.ShapeDtypeStruct((comps, pixels), BF),
        jax.ShapeDtypeStruct((comps, frames), BF),
        jax.ShapeDtypeStruct((nb, comps), F32),
    )
    results = pl.pallas_call(
        functools.partial(kernel, rows, cols),
        out_shape=out_shape,
        in_specs=[hbm] * 4 + [smem] * 2 + [hbm] * 2,
        out_specs=(vmem,) * 3,
        scratch_shapes=[
            pltpu.VMEM((pixels, frames), BF), pltpu.VMEM((comps, pixels), BF), pltpu.VMEM((comps, frames), BF),
            pltpu.VMEM((3, 1, slots), i32),
            pltpu.SMEM(row_int.shape, i32), pltpu.SMEM(col_int.shape, i32), pltpu.SemaphoreType.DMA((7,)),
            pltpu.VMEM((8, PAD, 2 * (pixels + frames)), BF), both, both,
            pltpu.VMEM((nbp, pixels), F32), pltpu.VMEM((frames, pixels), BF),
            pltpu.VMEM((nbp, pixels), BF), pltpu.VMEM((nbp, frames), BF),
            pltpu.VMEM((nbp, pixels), BF), pltpu.VMEM((nbp, frames), BF),
            pltpu.VMEM((slots, pixels), F32), pltpu.VMEM((slots, pixels), F32),
            pltpu.VMEM((slots, pixels), F32),
            pltpu.VMEM((nb, pixels), F32), pltpu.VMEM((nb, pixels), F32),
            pltpu.SemaphoreType.DMA((8,)), pltpu.SemaphoreType.DMA((2, 8)),
        ],
        compiler_params=pltpu.CompilerParams(
            collective_id=0, has_side_effects=True, vmem_limit_bytes=32 * 1024 * 1024),
    )(*[pltpu.with_memory_space_constraint(x, pltpu.HBM) for x in (
        residual[0, 0], footprints[0, 0], traces[0, 0], pairs)], pair_counts, comp_counts,
      *[pltpu.with_memory_space_constraint(x, pltpu.HBM) for x in (row_int, col_int)])
    foot, trace, corr = pl.pallas_call(
        store,
        out_shape=out_shape,
        in_specs=[vmem] * 3,
        out_specs=(hbm,) * 3,
        scratch_shapes=[pltpu.SemaphoreType.DMA((3,))],
        compiler_params=pltpu.CompilerParams(vmem_limit_bytes=4 * 1024 * 1024),
    )(*results)
    return foot[None, None], trace[None, None], jnp.transpose(corr)[None, None]


def solution(mesh):
    rows, cols = mesh.shape["py"], mesh.shape["px"]
    spec = P("py", "px", None, None)
    return jax.shard_map(
        functools.partial(shards, rows, cols), mesh=mesh,
        in_specs=(spec, spec, spec, spec, P("py", "px"), P("py", "px"), P(), P()),
        out_specs=(spec, spec, spec), check_vma=False)
```

time: 18.7 us -> 17.1 us (0.914)
  Pallas kernels: 16.5 us -> 15 us
    pallas_call x1, Pallas kernels: 15.7 us -> 14.2 us  [shards(): pl.pallas_call(functools.partial(kernel, rows, cols), out_shape=out_shape...]
where the time goes in v1:
time: 17.1 us; the launch traced here: 16.9 us
  Pallas kernels  15 us (88%)
  between operations  1.93 us (11%)
    pallas_call x1, Pallas kernels, shards(): pl.pallas_call(functools.partial(kernel, rows, cols), out_shape=out_shape...  14.2 us
    pallas_call x1, Pallas kernels, shards(): pl.pallas_call(store, out_shape=out_shape, in_specs=[vmem] * 3, out_specs...  0.76 us

profile of v1, /device:TPU:1, one launch (start us, length us, event | category | flops | bytes accessed | tf_op | source)
XLA Modules:
  0.0 16.9 jit_solution(2947405226999094848)
XLA Ops:
  1.9 14.2 %shard_map.103 = (bf16[40,4096]{1,0:T(8,128)(2,1)S(1)}, bf16[40,128]{1,0:T(8,128)(2,1)S(1)}, f32[24,40]{1,0:T(8,128)S(1)}) custom-call(bf16[4096,128]{1,0:T(8,128)(2,1)} %bitcast.11, bf16[40,4096]{1,0:T(8,128)(2,1)} %bitcast.12, bf16[40,128]{1,0:T(8,128)(2,1)} %bitcast.13, s32[3,1,16]{2,1,0:T(1,128)} %bitcast.14, s32[1,1]{1,0:T(1,128)S(6)} %copy.11.pair_count, ...), custom_call_target="tpu_custom_call" | custom-call | tf_op jit(solution)/shard_map/pallas_call | solution.py:427
  16.1 0.8 %shard_map.104 = (bf16[40,4096]{1,0:T(8,128)(2,1)}, bf16[40,128]{1,0:T(8,128)(2,1)}, f32[24,40]{1,0:T(8,128)}) custom-call(bf16[40,4096]{1,0:T(8,128)(2,1)S(1)} %get-tuple-element.9.foot, bf16[40,128]{1,0:T(8,128)(2,1)S(1)} %get-tuple-element.10.trace, f32[24,40]{1,0:T(8,128)S(1)} %get-tuple-element.11.corr), custom_call_target="tpu_custom_call" | custom-call | tf_op jit(solution)/shard_map/pallas_call | solution.py:450

commit v2 on v1

--- a/solution.py
+++ b/solution.py
@@ -80,7 +80,7 @@
     out_foot, out_trace, out_corr,
     res_ref, foot_ref, trace_ref, pair_ref, row_ref, col_ref, sem_in,
     send, recv1, recv2, wide, res_t,
-    border, border_trace, back, back_trace, a_own, a_rem, shape, take, keep,
+    border, border_trace, back, back_trace, a_own, a_rem, shape, feet, take, keep,
     sem_s, sem_r,
 ):
     pixels = foot_ref.shape[1]
@@ -128,18 +128,9 @@
         part = pl.ds(0, span1(d))
         return remote(send.at[d, :, part], recv1.at[7 - d, :, part], d, 0)
 
-    def copy2(d):
-        width = lanes_in(d, pixels)[1]
-        return remote(send.at[d, :, pl.ds(span1(d), width)], recv2.at[7 - d, :, pl.ds(0, width)], d, 1)
-
-    def copy3(d):
-        width = lanes_in(d, pixels)[1]
-        return remote(send.at[d, :, pl.ds(span1(d) + width, frames)],
-                      recv2.at[7 - d, :, pl.ds(width, frames)], d, 1)
-
     def both(d):
         part = pl.ds(0, span1(d))
-        return remote(send.at[d, :, part], recv2.at[7 - d, :, part], d, 1)
+        return remote(send.at[d, :, pl.ds(span1(d), span1(d))], recv2.at[7 - d, :, part], d, 1)
 
     def all_sent(d):
         part = send.at[d, :, pl.ds(0, 2 * span1(d))]
@@ -279,9 +270,7 @@
             border_trace[PAD * d:PAD * d + PAD, :] = recv1[d, :, width:width + frames]
 
     c_rem = dot(border_hot, border_trace[...])
-    for first in range(0, pixels, CHUNK):
-        span = slice(first, first + CHUNK)
-        a_rem[:, span] = dot(border_hot, border[:, span])
+    a_rem[...] = dot(border_hot, border[...])
 
     trace = c_own
     for t in range(ITERS):
@@ -289,7 +278,6 @@
         with_rem = jnp.sum(c_rem * trace, axis=1, keepdims=True)
         norm = 1.0 / (jnp.sum(trace * trace, axis=1, keepdims=True) + EPS * frames)
         trace_bf = trace.astype(BF)
-        down_sum = jnp.zeros((slots, frames), F32)
         sum_own = jnp.zeros((slots, LANES), F32)
         sum_rem = jnp.zeros((slots, LANES), F32)
         sum_sq = jnp.zeros((slots, LANES), F32)
@@ -305,20 +293,16 @@
             sum_own = sum_own + narrow(mine * foot)
             sum_rem = sum_rem + narrow(theirs * foot)
             sum_sq = sum_sq + narrow(foot * foot)
-            foot = foot.astype(BF)
-            down_sum = down_sum + dot(foot, res_ref[span, :])
-            if t == ITERS - 1:
-                shape[:, span] = foot.astype(F32)
+            feet[:, span] = foot.astype(BF)
+        if t == ITERS - 1:
+            for first in range(0, pixels, WIDE):
                 wide[:, first:first + WIDE] = lax.dot_general(
-                    border_hot, foot, (((0,), (0,)), ((), ())), preferred_element_type=F32)
+                    border_hot, feet[:, first:first + WIDE], (((0,), (0,)), ((), ())), preferred_element_type=F32)
+        down_sum = dot(feet[...], res_ref[...])
         if t == ITERS - 1:
             slid = {}
             for d in ORDER:
                 emit(d, span1(d), False, slid)
-            for d in ORDER:
-                @pl.when(exists(d))
-                def _():
-                    copy2(d).start()
         dot_own = jnp.sum(sum_own, axis=1, keepdims=True)
         dot_rem = jnp.sum(sum_rem, axis=1, keepdims=True)
         scale = 1.0 / (jnp.sum(sum_sq, axis=1, keepdims=True) + EPS * pixels)
@@ -333,7 +317,7 @@
     for d in ORDER:
         @pl.when(exists(d))
         def _():
-            copy3(d).start()
+            both(d).start()
 
     upper = slice(nb, comps)
     hot_up = own_hot[:, upper]
@@ -342,8 +326,7 @@
     alive_up = alive[upper]
     for first in range(0, pixels, CHUNK):
         span = slice(first, first + CHUNK)
-        new = lax.dot_general(hot_up, shape[:, span].astype(BF), (((0,), (0,)), ((), ())),
-                              preferred_element_type=F32)
+        new = lax.dot_general(hot_up, feet[:, span], (((0,), (0,)), ((), ())), preferred_element_type=F32)
         new = jnp.where(hit_up, new, foot_ref[upper, span].astype(F32))
         out_foot[upper, span] = jnp.where(alive_up, new, 0.0).astype(BF)
     new = lax.dot_general(hot_up, trace_bf, (((0,), (0,)), ((), ())), preferred_element_type=F32)
@@ -388,9 +371,10 @@
     out_trace[0:nb, :] = new.astype(BF)
     came = jnp.where(came, 1.0, 0.0)
     came = jnp.concatenate([came] * (CHUNK // LANES), axis=1)
+    wide[0:nb, :] = dot(squeeze, back[...])
     for first in range(0, pixels, CHUNK):
         span = slice(first, first + CHUNK)
-        new = dot(squeeze, back[:, span])
+        new = wide[0:nb, span]
         out_foot[0:nb, span] = jnp.where(take[:, span] * came > 0.5, new, keep[:, span]).astype(BF)
 
     for d in range(8):
@@ -438,7 +422,7 @@
             pltpu.VMEM((nbp, pixels), BF), pltpu.VMEM((nbp, frames), BF),
             pltpu.VMEM((nbp, pixels), BF), pltpu.VMEM((nbp, frames), BF),
             pltpu.VMEM((slots, pixels), F32), pltpu.VMEM((slots, pixels), F32),
-            pltpu.VMEM((slots, pixels), F32),
+            pltpu.VMEM((slots, pixels), F32), pltpu.VMEM((slots, pixels), BF),
             pltpu.VMEM((nb, pixels), F32), pltpu.VMEM((nb, pixels), F32),
             pltpu.SemaphoreType.DMA((8,)), pltpu.SemaphoreType.DMA((2, 8)),
         ],

time: 17.1 us -> 15.8 us (0.924)
  Pallas kernels: 15 us -> 13.6 us
    pallas_call x1, Pallas kernels: 14.2 us -> 12.8 us  [shards(): pl.pallas_call(functools.partial(kernel, rows, cols), out_shape=out_shape...]
where the time goes in v2:
time: 15.8 us; the launch traced here: 15.5 us
  Pallas kernels  13.6 us (86%)
  between operations  1.93 us (12%)
    pallas_call x1, Pallas kernels, shards(): pl.pallas_call(functools.partial(kernel, rows, cols), out_shape=out_shape...  12.8 us
    pallas_call x1, Pallas kernels, shards(): pl.pallas_call(store, out_shape=out_shape, in_specs=[vmem] * 3, out_specs...  0.76 us

profile of v2, /device:TPU:1, one launch (start us, length us, event | category | flops | bytes accessed | tf_op | source)
XLA Modules:
  0.0 15.5 jit_solution(10350684149087413648)
XLA Ops:
  1.9 12.8 %shard_map.103 = (bf16[40,4096]{1,0:T(8,128)(2,1)S(1)}, bf16[40,128]{1,0:T(8,128)(2,1)S(1)}, f32[24,40]{1,0:T(8,128)S(1)}) custom-call(bf16[4096,128]{1,0:T(8,128)(2,1)} %bitcast.11, bf16[40,4096]{1,0:T(8,128)(2,1)} %bitcast.12, bf16[40,128]{1,0:T(8,128)(2,1)} %bitcast.13, s32[3,1,16]{2,1,0:T(1,128)} %bitcast.14, s32[1,1]{1,0:T(1,128)S(6)} %copy.11.pair_count, ...), custom_call_target="tpu_custom_call" | custom-call | tf_op jit(solution)/shard_map/pallas_call | solution.py:411
  14.8 0.8 %shard_map.104 = (bf16[40,4096]{1,0:T(8,128)(2,1)}, bf16[40,128]{1,0:T(8,128)(2,1)}, f32[24,40]{1,0:T(8,128)}) custom-call(bf16[40,4096]{1,0:T(8,128)(2,1)S(1)} %get-tuple-element.9.foot, bf16[40,128]{1,0:T(8,128)(2,1)S(1)} %get-tuple-element.10.trace, f32[24,40]{1,0:T(8,128)S(1)} %get-tuple-element.11.corr), custom_call_target="tpu_custom_call" | custom-call | tf_op jit(solution)/shard_map/pallas_call | solution.py:434

commit v3 on v2

--- a/solution.py
+++ b/solution.py
@@ -57,16 +57,6 @@
     return functools.reduce(jnp.add, [x[:, b:b + LANES] for b in range(0, x.shape[1], LANES)])
 
 
-def shift_of(direction, up, down, left, right):
-    flat = direction + (direction >= 4).astype(jnp.int32)
-    row = (flat >= 3).astype(jnp.int32) + (flat >= 6).astype(jnp.int32)
-    dy = row - 1
-    dx = flat - 3 * row - 1
-    oy = jnp.where(dy < 0, up - PH, jnp.where(dy > 0, PH - down, 0))
-    ox = jnp.where(dx < 0, left - PW, jnp.where(dx > 0, PW - right, 0))
-    return oy, ox
-
-
 def inside_of(oy, ox, first, count):
     pixel = iota((1, count), 1) + first
     y = (pixel >> 6) - oy
@@ -78,9 +68,9 @@
     rows, cols,
     res_hbm, foot_hbm, trace_hbm, pair_hbm, pair_count, comp_count, row_hbm, col_hbm,
     out_foot, out_trace, out_corr,
-    res_ref, foot_ref, trace_ref, pair_ref, row_ref, col_ref, sem_in,
+    res_ref, foot_ref, trace_ref, pair_ref, row_ref, col_ref,
     send, recv1, recv2, wide, res_t,
-    border, border_trace, back, back_trace, a_own, a_rem, shape, feet, take, keep,
+    border, border_trace, a_own, a_rem, shape, feet, final, final_trace,
     sem_s, sem_r,
 ):
     pixels = foot_ref.shape[1]
@@ -100,7 +90,7 @@
         return (r >= 0) & (r < rows) & (c >= 0) & (c < cols)
 
     barrier = pltpu.get_barrier_semaphore()
-    for d in range(8):
+    for d in ORDER:
         @pl.when(exists(d))
         def _():
             pl.semaphore_signal(barrier, 1, device_id=target(d), device_id_type=MESH)
@@ -112,7 +102,7 @@
         (foot_hbm.at[pl.ds(nb, comps - nb)], foot_ref.at[pl.ds(nb, comps - nb)]),
         (res_hbm, res_ref),
     ]
-    fetches = [pltpu.make_async_copy(a, b, sem_in.at[i]) for i, (a, b) in enumerate(fetches)]
+    fetches = [pltpu.make_async_copy(a, b, sem_s.at[i]) for i, (a, b) in enumerate(fetches)]
     for fetch in fetches:
         fetch.start()
 
@@ -132,6 +122,13 @@
         part = pl.ds(0, span1(d))
         return remote(send.at[d, :, pl.ds(span1(d), span1(d))], recv2.at[7 - d, :, part], d, 1)
 
+    def issue(copy):
+        odd = (my_c & 1) == 1
+        for d, when in ((2, odd), (7, odd), (0, None), (5, None), (2, ~odd), (7, ~odd), (1, None), (6, None), (3, None), (4, None)):
+            @pl.when(exists(d) if when is None else exists(d) & when)
+            def _():
+                copy(d).start()
+
     def all_sent(d):
         part = send.at[d, :, pl.ds(0, 2 * span1(d))]
         return remote(part, part, d, 1)
@@ -140,8 +137,6 @@
     pick = (((j & (PAD - 1)) < NBR) & (iota((nbp, nb), 1) == NBR * (j >> 2) + (j & (PAD - 1)))).astype(BF)
     border[...] = jnp.zeros_like(border)
     border_trace[...] = jnp.zeros_like(border_trace)
-    back[...] = jnp.zeros_like(back)
-    back_trace[...] = jnp.zeros_like(back_trace)
     fetches[0].wait()
     own_traces = trace_ref[...]
     packed_traces = dot(pick, own_traces[0:nb])
@@ -211,17 +206,14 @@
     for d in ORDER:
         emit(d, 0, True, slid)
 
+    for fetch in fetches[4:]:
+        fetch.wait()
     total = jnp.int32(0)
     for d in range(8):
         total = total + exists(d).astype(jnp.int32)
     pl.semaphore_wait(barrier, total)
-    for d in ORDER:
-        @pl.when(exists(d))
-        def _():
-            copy1(d).start()
-
-    for fetch in fetches[4:]:
-        fetch.wait()
+    issue(copy1)
+
     same = iota((slots, slots), 0) == iota((slots, slots), 1)
 
     def column(values):
@@ -250,11 +242,8 @@
         shape[:, span] = dot(c_own_bf, turned) + mine * energy
 
     k = iota((nb, nbp), 0)
-    k_dir = iota((nb, 1), 0)
-    dir_of = jnp.zeros((nb, 1), jnp.int32)
     dir_wide = jnp.zeros((nb, nbp), jnp.int32)
     for d in range(1, 8):
-        dir_of = dir_of + (k_dir >= NBR * d).astype(jnp.int32)
         dir_wide = dir_wide + (k >= NBR * d).astype(jnp.int32)
     squeeze = (iota((nb, nbp), 1) == PAD * dir_wide + k - NBR * dir_wide).astype(BF)
     alive = iota((comps, 1), 0) < comp_count[0, 0]
@@ -314,10 +303,7 @@
     for d in range(8):
         first = span1(d) + lanes_in(d, pixels)[1]
         send[d, :, first:first + frames] = sent[PAD * d:PAD * d + PAD].astype(BF)
-    for d in ORDER:
-        @pl.when(exists(d))
-        def _():
-            both(d).start()
+    issue(both)
 
     upper = slice(nb, comps)
     hot_up = own_hot[:, upper]
@@ -345,37 +331,30 @@
     corr = cov / jnp.sqrt((spread_local + EPS) * (spread_remote + EPS))
     out_corr[...] = jnp.where(iota((1, comps), 1) < comp_count[0, 0], corr, 0.0)
 
-    oy, ox = shift_of(dir_of, up, down, left, right)
-    flat = dir_of + (dir_of >= 4).astype(jnp.int32)
-    row = (flat >= 3).astype(jnp.int32) + (flat >= 6).astype(jnp.int32)
-    dy = row - 1
-    dx = flat - 3 * row - 1
-    there = (my_r + dy >= 0) & (my_r + dy < rows) & (my_c + dx >= 0) & (my_c + dx < cols) & alive_low
     for first in range(0, pixels, CHUNK):
         span = slice(first, first + CHUNK)
-        take[:, span] = jnp.where(inside_of(oy, ox, first, CHUNK) & there, 1.0, 0.0)
-        keep[:, span] = jnp.where(alive_low, foot_ref[0:nb, span].astype(F32), 0.0)
-
+        final[:, span] = foot_ref[0:nb, span].astype(F32)
+    final_trace[...] = own_traces[0:nb].astype(F32)
     for d in RECEIVE:
         start, width = lanes_out(d, pixels)
+        oy, ox = offsets(d)
+        part = slice(NBR * d, NBR * d + NBR)
 
         @pl.when(exists(d))
         def _():
             both(7 - d).wait_recv()
-            back[PAD * d:PAD * d + PAD, start:start + width] = recv2[d, :, 0:width]
-            back_trace[PAD * d:PAD * d + PAD, :] = recv2[d, :, width:width + frames]
-
-    new = dot(squeeze, back_trace[...])
-    came = new >= 0.0
-    new = jnp.where(there & came, new, jnp.where(alive_low, own_traces[0:nb].astype(F32), 0.0))
-    out_trace[0:nb, :] = new.astype(BF)
-    came = jnp.where(came, 1.0, 0.0)
-    came = jnp.concatenate([came] * (CHUNK // LANES), axis=1)
-    wide[0:nb, :] = dot(squeeze, back[...])
+            new = recv2[d, :, width:width + frames].astype(F32)[0:NBR]
+            came = new >= 0.0
+            final_trace[part, :] = jnp.where(came, new, final_trace[part, :])
+            for first in range(0, width, LANES):
+                span = slice(start + first, start + first + LANES)
+                new = recv2[d, :, first:first + LANES].astype(F32)[0:NBR]
+                final[part, span] = jnp.where(came & inside_of(oy, ox, start + first, LANES), new, final[part, span])
+
+    out_trace[0:nb, :] = jnp.where(alive_low, final_trace[...], 0.0).astype(BF)
     for first in range(0, pixels, CHUNK):
         span = slice(first, first + CHUNK)
-        new = wide[0:nb, span]
-        out_foot[0:nb, span] = jnp.where(take[:, span] * came > 0.5, new, keep[:, span]).astype(BF)
+        out_foot[0:nb, span] = jnp.where(alive_low, final[:, span], 0.0).astype(BF)
 
     for d in range(8):
         @pl.when(exists(d))
@@ -416,14 +395,13 @@
         scratch_shapes=[
             pltpu.VMEM((pixels, frames), BF), pltpu.VMEM((comps, pixels), BF), pltpu.VMEM((comps, frames), BF),
             pltpu.VMEM((3, 1, slots), i32),
-            pltpu.SMEM(row_int.shape, i32), pltpu.SMEM(col_int.shape, i32), pltpu.SemaphoreType.DMA((7,)),
+            pltpu.SMEM(row_int.shape, i32), pltpu.SMEM(col_int.shape, i32),
             pltpu.VMEM((8, PAD, 2 * (pixels + frames)), BF), both, both,
             pltpu.VMEM((nbp, pixels), F32), pltpu.VMEM((frames, pixels), BF),
             pltpu.VMEM((nbp, pixels), BF), pltpu.VMEM((nbp, frames), BF),
-            pltpu.VMEM((nbp, pixels), BF), pltpu.VMEM((nbp, frames), BF),
             pltpu.VMEM((slots, pixels), F32), pltpu.VMEM((slots, pixels), F32),
             pltpu.VMEM((slots, pixels), F32), pltpu.VMEM((slots, pixels), BF),
-            pltpu.VMEM((nb, pixels), F32), pltpu.VMEM((nb, pixels), F32),
+            pltpu.VMEM((nb, pixels), F32), pltpu.VMEM((nb, frames), F32),
             pltpu.SemaphoreType.DMA((8,)), pltpu.SemaphoreType.DMA((2, 8)),
         ],
         compiler_params=pltpu.CompilerParams(

time: 15.8 us -> 15.7 us (level)
  no operation moved by 1% of the time
where the time goes in v3:
time: 15.7 us; the launch traced here: 15.5 us
  Pallas kernels  13.5 us (86%)
  between operations  1.93 us (12%)
    pallas_call x1, Pallas kernels, shards(): pl.pallas_call(functools.partial(kernel, rows, cols), out_shape=out_shape...  12.8 us
    pallas_call x1, Pallas kernels, shards(): pl.pallas_call(store, out_shape=out_shape, in_specs=[vmem] * 3, out_specs...  0.76 us

profile of v3, /device:TPU:1, one launch (start us, length us, event | category | flops | bytes accessed | tf_op | source)
XLA Modules:
  0.0 15.5 jit_solution(3991732366738924171)
XLA Ops:
  1.9 12.8 %shard_map.103 = (bf16[40,4096]{1,0:T(8,128)(2,1)S(1)}, bf16[40,128]{1,0:T(8,128)(2,1)S(1)}, f32[24,40]{1,0:T(8,128)S(1)}) custom-call(bf16[4096,128]{1,0:T(8,128)(2,1)} %bitcast.11, bf16[40,4096]{1,0:T(8,128)(2,1)} %bitcast.12, bf16[40,128]{1,0:T(8,128)(2,1)} %bitcast.13, s32[3,1,16]{2,1,0:T(1,128)} %bitcast.14, s32[1,1]{1,0:T(1,128)S(6)} %copy.11.pair_count, ...), custom_call_target="tpu_custom_call" | custom-call | tf_op jit(solution)/shard_map/pallas_call | solution.py:390
  14.7 0.8 %shard_map.104 = (bf16[40,4096]{1,0:T(8,128)(2,1)}, bf16[40,128]{1,0:T(8,128)(2,1)}, f32[24,40]{1,0:T(8,128)}) custom-call(bf16[40,4096]{1,0:T(8,128)(2,1)S(1)} %get-tuple-element.9.foot, bf16[40,128]{1,0:T(8,128)(2,1)S(1)} %get-tuple-element.10.trace, f32[24,40]{1,0:T(8,128)S(1)} %get-tuple-element.11.corr), custom_call_target="tpu_custom_call" | custom-call | tf_op jit(solution)/shard_map/pallas_call | solution.py:412

commit v4 on v3

--- a/solution.py
+++ b/solution.py
@@ -70,7 +70,7 @@
     out_foot, out_trace, out_corr,
     res_ref, foot_ref, trace_ref, pair_ref, row_ref, col_ref,
     send, recv1, recv2, wide, res_t,
-    border, border_trace, a_own, a_rem, shape, feet, final, final_trace,
+    border_trace, c_rem_ref, a_own, a_rem, shape, feet, final, final_trace,
     sem_s, sem_r,
 ):
     pixels = foot_ref.shape[1]
@@ -135,7 +135,8 @@
 
     j = iota((nbp, nb), 0)
     pick = (((j & (PAD - 1)) < NBR) & (iota((nbp, nb), 1) == NBR * (j >> 2) + (j & (PAD - 1)))).astype(BF)
-    border[...] = jnp.zeros_like(border)
+    a_rem[...] = jnp.zeros_like(a_rem)
+    c_rem_ref[...] = jnp.zeros_like(c_rem_ref)
     border_trace[...] = jnp.zeros_like(border_trace)
     fetches[0].wait()
     own_traces = trace_ref[...]
@@ -229,6 +230,8 @@
     border_hot = ((iota((slots, nbp), 1) == border_slot) & live).astype(BF)
     hit = lax.dot_general(border_hot, jnp.ones((slots, LANES), BF), (((0,), (0,)), ((), ())),
                           preferred_element_type=F32) > 0.5
+    slot_of = lax.dot_general(border_hot, iota((slots, LANES), 0).astype(BF), (((0,), (0,)), ((), ())),
+                              preferred_element_type=F32).astype(jnp.int32)
 
     c_own = dot(own_hot, own_traces)
     c_own_bf = c_own.astype(BF)
@@ -249,17 +252,36 @@
     alive = iota((comps, 1), 0) < comp_count[0, 0]
     alive_low = alive[0:nb]
 
+    place_wide = jnp.broadcast_to(place & (PAD - 1), (slots, LANES))
+    direction_wide = jnp.broadcast_to(jnp.where(live, direction, -1), (slots, LANES))
+
+    def gather(d, first, to, span):
+        got = recv1[d, :, first:first + LANES].astype(F32)
+        got = jnp.concatenate([got, got], axis=0)
+        for low in range(0, slots, 8):
+            part = slice(low, low + 8)
+            row = jnp.take_along_axis(got, place_wide[part], axis=0)
+            to[part, span] = jnp.where(direction_wide[part] == d, row, to[part, span])
+
     for d in RECEIVE:
         start, width = lanes_out(d, pixels)
 
         @pl.when(exists(d))
         def _():
             copy1(7 - d).wait_recv()
-            border[PAD * d:PAD * d + PAD, start:start + width] = recv1[d, :, 0:width]
+            gather(d, width, c_rem_ref, slice(0, frames))
+            for first in range(0, width, LANES):
+                gather(d, first, a_rem, slice(start + first, start + first + LANES))
             border_trace[PAD * d:PAD * d + PAD, :] = recv1[d, :, width:width + frames]
 
-    c_rem = dot(border_hot, border_trace[...])
-    a_rem[...] = dot(border_hot, border[...])
+    c_rem = c_rem_ref[...]
+
+    def choose(values, low):
+        at = slot_of[low:low + 8]
+        row = jnp.take_along_axis(values[0:8], at & 7, axis=0)
+        for first in range(8, slots, 8):
+            row = jnp.where(at >= first, jnp.take_along_axis(values[first:first + 8], at & 7, axis=0), row)
+        return row
 
     trace = c_own
     for t in range(ITERS):
@@ -284,9 +306,13 @@
             sum_sq = sum_sq + narrow(foot * foot)
             feet[:, span] = foot.astype(BF)
         if t == ITERS - 1:
-            for first in range(0, pixels, WIDE):
-                wide[:, first:first + WIDE] = lax.dot_general(
-                    border_hot, feet[:, first:first + WIDE], (((0,), (0,)), ((), ())), preferred_element_type=F32)
+            for low in range(0, nbp, 8):
+                rows_of = [STEPS[d][0] for d in (low // PAD, low // PAD + 1)]
+                begin = 0 if min(rows_of) <= 0 else pixels - STRIP
+                end = pixels if max(rows_of) >= 0 else STRIP
+                for first in range(begin, end, LANES):
+                    span = slice(first, first + LANES)
+                    wide[low:low + 8, span] = choose(feet[:, span].astype(F32), low)
         down_sum = dot(feet[...], res_ref[...])
         if t == ITERS - 1:
             slid = {}
@@ -298,8 +324,7 @@
         trace = jnp.maximum(down_sum + c_own * dot_own + c_rem * dot_rem, 0.0) * scale
 
     trace_bf = trace.astype(BF)
-    sent = lax.dot_general(border_hot, trace_bf, (((0,), (0,)), ((), ())), preferred_element_type=F32)
-    sent = jnp.where(hit, sent, -1.0)
+    sent = jnp.where(hit, jnp.concatenate([choose(trace, low) for low in range(0, nbp, 8)], axis=0), -1.0)
     for d in range(8):
         first = span1(d) + lanes_in(d, pixels)[1]
         send[d, :, first:first + frames] = sent[PAD * d:PAD * d + PAD].astype(BF)
@@ -398,7 +423,7 @@
             pltpu.SMEM(row_int.shape, i32), pltpu.SMEM(col_int.shape, i32),
             pltpu.VMEM((8, PAD, 2 * (pixels + frames)), BF), both, both,
             pltpu.VMEM((nbp, pixels), F32), pltpu.VMEM((frames, pixels), BF),
-            pltpu.VMEM((nbp, pixels), BF), pltpu.VMEM((nbp, frames), BF),
+            pltpu.VMEM((nbp, frames), BF), pltpu.VMEM((slots, frames), F32),
             pltpu.VMEM((slots, pixels), F32), pltpu.VMEM((slots, pixels), F32),
             pltpu.VMEM((slots, pixels), F32), pltpu.VMEM((slots, pixels), BF),
             pltpu.VMEM((nb, pixels), F32), pltpu.VMEM((nb, frames), F32),

time: 15.7 us -> 15.4 us (0.981)
  Pallas kernels: 13.5 us -> 13.2 us
    pallas_call x1, Pallas kernels: 12.8 us -> 12.5 us  [shards(): pl.pallas_call(functools.partial(kernel, rows, cols), out_shape=out_shape...]
where the time goes in v4:
time: 15.4 us; the launch traced here: 15.2 us
  Pallas kernels  13.2 us (86%)
  between operations  1.93 us (13%)
    pallas_call x1, Pallas kernels, shards(): pl.pallas_call(functools.partial(kernel, rows, cols), out_shape=out_shape...  12.5 us
    pallas_call x1, Pallas kernels, shards(): pl.pallas_call(store, out_shape=out_shape, in_specs=[vmem] * 3, out_specs...  0.76 us

profile of v4, /device:TPU:1, one launch (start us, length us, event | category | flops | bytes accessed | tf_op | source)
XLA Modules:
  0.0 15.2 jit_solution(8572901641870546024)
XLA Ops:
  1.9 12.5 %shard_map.103 = (bf16[40,4096]{1,0:T(8,128)(2,1)S(1)}, bf16[40,128]{1,0:T(8,128)(2,1)S(1)}, f32[24,40]{1,0:T(8,128)S(1)}) custom-call(bf16[4096,128]{1,0:T(8,128)(2,1)} %bitcast.11, bf16[40,4096]{1,0:T(8,128)(2,1)} %bitcast.12, bf16[40,128]{1,0:T(8,128)(2,1)} %bitcast.13, s32[3,1,16]{2,1,0:T(1,128)} %bitcast.14, s32[1,1]{1,0:T(1,128)S(6)} %copy.11.pair_count, ...), custom_call_target="tpu_custom_call" | custom-call | tf_op jit(solution)/shard_map/pallas_call | solution.py:415
  14.4 0.8 %shard_map.104 = (bf16[40,4096]{1,0:T(8,128)(2,1)}, bf16[40,128]{1,0:T(8,128)(2,1)}, f32[24,40]{1,0:T(8,128)}) custom-call(bf16[40,4096]{1,0:T(8,128)(2,1)S(1)} %get-tuple-element.9.foot, bf16[40,128]{1,0:T(8,128)(2,1)S(1)} %get-tuple-element.10.trace, f32[24,40]{1,0:T(8,128)S(1)} %get-tuple-element.11.corr), custom_call_target="tpu_custom_call" | custom-call | tf_op jit(solution)/shard_map/pallas_call | solution.py:437

commit v5 on v4

--- a/solution.py
+++ b/solution.py
@@ -21,7 +21,8 @@
 LANES = 128
 LOW = (PH - OV_HI) // 2
 ORDER = (0, 2, 5, 7, 1, 6, 3, 4)
-RECEIVE = (3, 4, 1, 6, 0, 2, 5, 7)
+ISSUE = ((2, 1), (7, 1), (0, None), (5, None), (2, 0), (7, 0), (1, None), (6, None), (3, None), (4, None))
+RECEIVE = ((3, None), (4, None), (1, None), (6, None), (0, 1), (5, 1), (2, 0), (7, 0), (0, 0), (5, 0), (2, 1), (7, 1))
 STEPS = [(-1, -1), (-1, 0), (-1, 1), (0, -1), (0, 1), (1, -1), (1, 0), (1, 1)]
 BF = jnp.bfloat16
 F32 = jnp.float32
@@ -71,7 +72,7 @@
     res_ref, foot_ref, trace_ref, pair_ref, row_ref, col_ref,
     send, recv1, recv2, wide, res_t,
     border_trace, c_rem_ref, a_own, a_rem, shape, feet, final, final_trace,
-    sem_s, sem_r,
+    sem_s, sem_r, sem_f,
 ):
     pixels = foot_ref.shape[1]
     frames = trace_ref.shape[1]
@@ -89,9 +90,12 @@
         r, c = target(d)
         return (r >= 0) & (r < rows) & (c >= 0) & (c < cols)
 
+    def now(d, parity):
+        return exists(d) if parity is None else exists(d) & ((my_c & 1) == parity)
+
     barrier = pltpu.get_barrier_semaphore()
-    for d in ORDER:
-        @pl.when(exists(d))
+    for d, parity in ISSUE:
+        @pl.when(now(d, parity))
         def _():
             pl.semaphore_signal(barrier, 1, device_id=target(d), device_id_type=MESH)
     fetches = [
@@ -102,7 +106,7 @@
         (foot_hbm.at[pl.ds(nb, comps - nb)], foot_ref.at[pl.ds(nb, comps - nb)]),
         (res_hbm, res_ref),
     ]
-    fetches = [pltpu.make_async_copy(a, b, sem_s.at[i]) for i, (a, b) in enumerate(fetches)]
+    fetches = [pltpu.make_async_copy(a, b, sem_s.at[i] if i < 6 else sem_f.at[0]) for i, (a, b) in enumerate(fetches)]
     for fetch in fetches:
         fetch.start()
 
@@ -123,9 +127,8 @@
         return remote(send.at[d, :, pl.ds(span1(d), span1(d))], recv2.at[7 - d, :, part], d, 1)
 
     def issue(copy):
-        odd = (my_c & 1) == 1
-        for d, when in ((2, odd), (7, odd), (0, None), (5, None), (2, ~odd), (7, ~odd), (1, None), (6, None), (3, None), (4, None)):
-            @pl.when(exists(d) if when is None else exists(d) & when)
+        for d, parity in ISSUE:
+            @pl.when(now(d, parity))
             def _():
                 copy(d).start()
 
@@ -200,14 +203,31 @@
         for b in range(blocks):
             send[d, :, first + LANES * b:first + LANES * (b + 1)] = stack[8 * b + low:8 * b + low + PAD].astype(BF)
 
+    def pack(values, low):
+        j = iota((8, LANES), 0)
+        comp = (low // PAD) * NBR + NBR * (j >> 2) + jnp.minimum(j & (PAD - 1), NBR - 1)
+        begin = (low // PAD) * NBR // 8 * 8
+        row = jnp.take_along_axis(values[begin:begin + 8], comp & 7, axis=0)
+        if begin + 8 < (low // PAD) * NBR + 2 * NBR:
+            row = jnp.where(comp >= begin + 8, jnp.take_along_axis(values[begin + 8:begin + 16], comp & 7, axis=0), row)
+        return row
+
+    def spread(read, pick_rows):
+        for low in range(0, nbp, 8):
+            steps = [STEPS[d][0] for d in (low // PAD, low // PAD + 1)]
+            begin = 0 if min(steps) <= 0 else pixels - STRIP
+            end = pixels if max(steps) >= 0 else STRIP
+            for first in range(begin, end, LANES):
+                span = slice(first, first + LANES)
+                wide[low:low + 8, span] = pick_rows(read(span), low)
+
     fetches[3].wait()
-    for first in range(0, pixels, CHUNK):
-        wide[:, first:first + CHUNK] = dot(pick, foot_ref[0:nb, first:first + CHUNK])
+    spread(lambda span: foot_ref[0:nb, span].astype(F32), pack)
     slid = {}
     for d in ORDER:
         emit(d, 0, True, slid)
 
-    for fetch in fetches[4:]:
+    for fetch in fetches[4:6]:
         fetch.wait()
     total = jnp.int32(0)
     for d in range(8):
@@ -233,6 +253,7 @@
     slot_of = lax.dot_general(border_hot, iota((slots, LANES), 0).astype(BF), (((0,), (0,)), ((), ())),
                               preferred_element_type=F32).astype(jnp.int32)
 
+    fetches[6].wait()
     c_own = dot(own_hot, own_traces)
     c_own_bf = c_own.astype(BF)
     energy = jnp.sum(c_own * c_own, axis=1, keepdims=True)
@@ -263,10 +284,10 @@
             row = jnp.take_along_axis(got, place_wide[part], axis=0)
             to[part, span] = jnp.where(direction_wide[part] == d, row, to[part, span])
 
-    for d in RECEIVE:
+    for d, parity in RECEIVE:
         start, width = lanes_out(d, pixels)
 
-        @pl.when(exists(d))
+        @pl.when(now(d, parity))
         def _():
             copy1(7 - d).wait_recv()
             gather(d, width, c_rem_ref, slice(0, frames))
@@ -306,13 +327,7 @@
             sum_sq = sum_sq + narrow(foot * foot)
             feet[:, span] = foot.astype(BF)
         if t == ITERS - 1:
-            for low in range(0, nbp, 8):
-                rows_of = [STEPS[d][0] for d in (low // PAD, low // PAD + 1)]
-                begin = 0 if min(rows_of) <= 0 else pixels - STRIP
-                end = pixels if max(rows_of) >= 0 else STRIP
-                for first in range(begin, end, LANES):
-                    span = slice(first, first + LANES)
-                    wide[low:low + 8, span] = choose(feet[:, span].astype(F32), low)
+            spread(lambda span: feet[:, span].astype(F32), choose)
         down_sum = dot(feet[...], res_ref[...])
         if t == ITERS - 1:
             slid = {}
@@ -360,12 +375,12 @@
         span = slice(first, first + CHUNK)
         final[:, span] = foot_ref[0:nb, span].astype(F32)
     final_trace[...] = own_traces[0:nb].astype(F32)
-    for d in RECEIVE:
+    for d, parity in RECEIVE:
         start, width = lanes_out(d, pixels)
         oy, ox = offsets(d)
         part = slice(NBR * d, NBR * d + NBR)
 
-        @pl.when(exists(d))
+        @pl.when(now(d, parity))
         def _():
             both(7 - d).wait_recv()
             new = recv2[d, :, width:width + frames].astype(F32)[0:NBR]
@@ -427,7 +442,7 @@
             pltpu.VMEM((slots, pixels), F32), pltpu.VMEM((slots, pixels), F32),
             pltpu.VMEM((slots, pixels), F32), pltpu.VMEM((slots, pixels), BF),
             pltpu.VMEM((nb, pixels), F32), pltpu.VMEM((nb, frames), F32),
-            pltpu.SemaphoreType.DMA((8,)), pltpu.SemaphoreType.DMA((2, 8)),
+            pltpu.SemaphoreType.DMA((8,)), pltpu.SemaphoreType.DMA((2, 8)), pltpu.SemaphoreType.DMA((1,)),
         ],
         compiler_params=pltpu.CompilerParams(
             collective_id=0, has_side_effects=True, vmem_limit_bytes=32 * 1024 * 1024),

time: 15.4 us -> 15.5 us (level)
  no operation moved by 1% of the time
where the time goes in v5:
time: 15.5 us; the launch traced here: 15.3 us
  Pallas kernels  13.3 us (86%)
  between operations  1.93 us (12%)
    pallas_call x1, Pallas kernels, shards(): pl.pallas_call(functools.partial(kernel, rows, cols), out_shape=out_shape...  12.6 us
    pallas_call x1, Pallas kernels, shards(): pl.pallas_call(store, out_shape=out_shape, in_specs=[vmem] * 3, out_specs...  0.76 us

profile of v5, /device:TPU:1, one launch (start us, length us, event | category | flops | bytes accessed | tf_op | source)
XLA Modules:
  0.0 15.3 jit_solution(17285798853476294998)
XLA Ops:
  1.9 12.6 %shard_map.103 = (bf16[40,4096]{1,0:T(8,128)(2,1)S(1)}, bf16[40,128]{1,0:T(8,128)(2,1)S(1)}, f32[24,40]{1,0:T(8,128)S(1)}) custom-call(bf16[4096,128]{1,0:T(8,128)(2,1)} %bitcast.11, bf16[40,4096]{1,0:T(8,128)(2,1)} %bitcast.12, bf16[40,128]{1,0:T(8,128)(2,1)} %bitcast.13, s32[3,1,16]{2,1,0:T(1,128)} %bitcast.14, s32[1,1]{1,0:T(1,128)S(6)} %copy.11.pair_count, ...), custom_call_target="tpu_custom_call" | custom-call | tf_op jit(solution)/shard_map/pallas_call | solution.py:430
  14.5 0.8 %shard_map.104 = (bf16[40,4096]{1,0:T(8,128)(2,1)}, bf16[40,128]{1,0:T(8,128)(2,1)}, f32[24,40]{1,0:T(8,128)}) custom-call(bf16[40,4096]{1,0:T(8,128)(2,1)S(1)} %get-tuple-element.9.foot, bf16[40,128]{1,0:T(8,128)(2,1)S(1)} %get-tuple-element.10.trace, f32[24,40]{1,0:T(8,128)S(1)} %get-tuple-element.11.corr), custom_call_target="tpu_custom_call" | custom-call | tf_op jit(solution)/shard_map/pallas_call | solution.py:452
